TPU v7x, 64 devices: a 2x2x8 block of a 4x4x8 slice. The times are simulated.
64 devices in a mesh: dp: 8 (over x, y, core), tp: 8 (over z).
Axes of the slice: x: 2, y: 2, z: 8, core: 2. Of those that a mesh axis runs over, the one named last changes fastest.
The devices are a block of a 4x4x8 slice.
Arguments:
- x: bfloat16 [1024, 5120], P('dp'), parts along dimension 0
- w_gate: bfloat16 [5120, 27648], P(None, 'tp')
- w_up: bfloat16 [5120, 27648], P(None, 'tp')
- w_down: bfloat16 [27648, 5120], P('tp')
Outputs:
- output: bfloat16 [1024, 5120], P('dp'), parts along dimension 0
There are 8 independent parts. A program takes and returns all parts, laid end to end along the dimension named above; an argument that names none is the same for every part.
All inputs are finite; a program needn't handle non-finite values.
Results may differ from a plain program's by a relative error of at most 0.016.
Values are sent between devices in bfloat16 or wider.
A program may use at most 768 MiB of HBM per device.

v0:
```python
import jax
import jax.numpy as jnp
from jax import lax
from jax.sharding import PartitionSpec as P


def solution(mesh):
    def step(x, w_gate, w_up, w_down):
        gate = jnp.dot(x, w_gate, preferred_element_type=jnp.float32)
        up = jnp.dot(x, w_up, preferred_element_type=jnp.float32)
        hidden = (jax.nn.silu(gate) * up).astype(jnp.bfloat16)
        term = jnp.dot(hidden, w_down, preferred_element_type=jnp.float32).astype(jnp.bfloat16)
        return lax.psum(term, "tp")

    return jax.shard_map(
        step,
        mesh=mesh,
        in_specs=(P("dp", None), P(None, "tp"), P(None, "tp"), P("tp", None)),
        out_specs=P("dp", None),
        check_vma=False,
    )
```

profile of v0, /device:TPU:22, one launch (start us, length us, event | category | flops | bytes accessed | tf_op | source)
XLA Modules:
  0.0 132.1 jit_solution(9105178040248093875)
XLA Ops:
  6.5 0.0 copy-start
  6.6 0.0 all-reduce.2.cloned.1.call-start
  6.6 1.3 copy-done
  7.9 13.6 %fusion.1 = f32[128,3456]{1,0:T(8,128)S(1)} fusion(bf16[128,5120]{1,0:T(8,128)(2,1)S(1)} %copy-done, bf16[5120,3456]{1,0:T(8,128)(2,1)} %param.5), kind=kOutput, calls=%fused_computation.3 | convolution fusion | flops 4529848320 | bytes 38469632 | tf_op jit(solution)/shard_map/dot_general | solution.py:9
  21.5 26.3 %convolution_convert_fusion = bf16[128,5120]{1,0:T(8,128)(2,1)} fusion(bf16[3456,5120]{1,0:T(8,128)(2,1)} %param.7, bf16[128,5120]{1,0:T(8,128)(2,1)S(1)} %copy-done, bf16[5120,3456]{1,0:T(8,128)(2,1)} %param.6, f32[128,3456]{1,0:T(8,128)S(1)} %fusion.1), kind=kOutput, calls=%fused_computation | convolution fusion | flops 9063006208 | bytes 75169792 | tf_op jit(solution)/shard_map/dot_general | solution.py:12
  47.9 0.0 copy-start.1
  47.9 0.1 all-reduce.2.cloned.1.call-update
  47.9 74.8 %all-reduce.2.cloned.1.call-done = bf16[128,5120]{1,0:T(8,128)(2,1)} async-done(((bf16[128,5120]{1,0:T(8,128)(2,1)}), bf16[128,5120]{1,0:T(8,128)(2,1)}) %all-reduce.2.cloned.1.call-update) | async-done | bytes 1310736 | tf_op jit(solution)/shard_map/psum | solution.py:13
  122.7 2.5 %copy.6 = bf16[128,5120]{1,0:T(8,128)(2,1)} copy(bf16[128,5120]{1,0:T(8,128)(2,1)} %all-reduce.2.cloned.1.call-done) | data formatting | bytes 2621440
  125.2 0.0 copy-done.1
Async XLA Ops:
  6.5 1.3 copy-start
  6.6 116.2 %all-reduce.2.cloned.1.call-start = ((), (), s32[]{:S(2)}) async-start(), calls=%async_computation | async-start | bytes 2621440 | tf_op jit(solution)/shard_map/psum | solution.py:13
  47.9 77.3 %copy-start.1 = (bf16[128,5120]{1,0:T(8,128)(2,1)S(1)}, bf16[128,5120]{1,0:T(8,128)(2,1)}, u32[]{:S(2)}) copy-start(bf16[128,5120]{1,0:T(8,128)(2,1)} %param.4) | copy-start | bytes 3932164
Sparse Core Ops, SparseCore 0:
  48.0 74.6 all-reduce.1
where the time goes:
time: 132 us
  waiting for transfers between devices  74.9 us (57%)
  matrix products  40 us (30%)
  between operations  13.4 us (10%)
  local copies, waits for them, and re-layouts  3.77 us (3%)
    psum x1, waiting for transfers between devices, step(): return lax.psum(term, 'tp')  74.8 us
    dot_general x1, matrix products, step(): jnp.dot(hidden, w_down, preferred_element_type=jnp.float32)  26.3 us
    dot_general x1, matrix products, step(): gate = jnp.dot(x, w_gate, preferred_element_type=jnp.float32)  13.6 us
    unnamed x5, local copies, waits for them, and re-layouts  3.77 us
  transfers between devices with their start and end apart: 1, of which 1 were waited for; matrix products, arithmetic and copies ran while one was open for 0% of the time, Pallas kernels for 0%

commit v1 on v0

v1 whole, which is shorter than its diff:
```python
import functools

import jax
import jax.numpy as jnp
from jax import lax
from jax.experimental import pallas as pl
from jax.experimental.pallas import tpu as pltpu
from jax.sharding import PartitionSpec as P

AXIS = "tp"
SLAB = 256
SLOTS = 3
CHUNKS = 4
LEFT, RIGHT = 0, 1


def kernel(n, x_hbm, g_hbm, u_hbm, d_hbm, out, xb, gb, ub, wd, hid, term, sbuf, rbuf,
           x_sem, g_sem, u_sem, d_sem, send_sem, rs_sem, ag_sem):
    rows, width = x_hbm.shape[0], d_hbm.shape[1] // n
    depth = g_hbm.shape[1]
    full, rest = depth // SLAB, depth % SLAB
    half = n // 2
    me = lax.axis_index(AXIS)
    near = {LEFT: lax.rem(me + n - 1, n), RIGHT: lax.rem(me + 1, n)}
    cr = rows // CHUNKS

    def at(offset):
        return lax.rem(me + offset + n, n)

    def slab(i, slot, size=SLAB):
        cols = pl.ds(pl.multiple_of(i * SLAB, 128), size)
        dst = (slot, slice(None), pl.ds(0, size))
        return (
            pltpu.make_async_copy(g_hbm.at[:, cols], gb.at[dst], g_sem.at[slot]),
            pltpu.make_async_copy(u_hbm.at[:, cols], ub.at[dst], u_sem.at[slot]),
        )

    order = [half]
    for k in range(half - 1, 0, -1):
        order += [-k, k]
    order += [0]
    place = {o: b for b, o in enumerate(order)}

    def down(b):
        cols = pl.ds(pl.multiple_of(at(order[b]) * width, 128), width)
        return pltpu.make_async_copy(d_hbm.at[:, cols], wd.at[b], d_sem.at[b])

    x_copy = pltpu.make_async_copy(x_hbm, xb, x_sem)
    x_copy.start()
    for i in range(min(SLOTS, full)):
        for c in slab(i, i):
            c.start()

    barrier = pltpu.get_barrier_semaphore()
    for side in (LEFT, RIGHT):
        pl.semaphore_signal(barrier, inc=1, device_id={AXIS: near[side]}, device_id_type=pl.DeviceIdType.MESH)

    x_copy.wait()

    def hidden(i, slot, size):
        for c in slab(i, slot, size):
            c.wait()
        x = xb[...]
        gate = jnp.dot(x, gb[slot, :, :size], preferred_element_type=jnp.float32)
        up = jnp.dot(x, ub[slot, :, :size], preferred_element_type=jnp.float32)
        cols = pl.ds(pl.multiple_of(i * SLAB, 128), size)
        hid[:, cols] = (jax.nn.silu(gate) * up).astype(jnp.bfloat16)

    @pl.loop(0, full)
    def _(i):
        slot = lax.rem(i, SLOTS)
        hidden(i, slot, SLAB)

        @pl.when(i + SLOTS < full)
        def _():
            for c in slab(i + SLOTS, slot):
                c.start()

        if rest:
            @pl.when(i + SLOTS == full)
            def _():
                for c in slab(full, full % SLOTS, rest):
                    c.start()
                down(0).start()

        for b in range(1, SLOTS):
            @pl.when(i + SLOTS == full + b)
            def _():
                down(b).start()

    for b in range(SLOTS, n):
        down(b).start()
    if rest:
        hidden(full, full % SLOTS, rest)

    def chunk(c):
        return pl.ds(c * cr, cr)

    def sum_copy(side, step, c):
        return pltpu.make_async_remote_copy(
            src_ref=sbuf.at[side, step, chunk(c)],
            dst_ref=rbuf.at[side, step, chunk(c)],
            send_sem=send_sem.at[0, side, step],
            recv_sem=rs_sem.at[side, step, c],
            device_id={AXIS: near[side]},
            device_id_type=pl.DeviceIdType.MESH,
        )

    def gather_copy(side, step, c):
        owner = at(step if side == LEFT else -step)
        ref = out.at[chunk(c), pl.ds(pl.multiple_of(owner * width, 128), width)]
        return pltpu.make_async_remote_copy(
            src_ref=ref,
            dst_ref=ref,
            send_sem=send_sem.at[1, side, step],
            recv_sem=ag_sem.at[side, step, c],
            device_id={AXIS: near[side]},
            device_id_type=pl.DeviceIdType.MESH,
        )

    def arrived(side, step, c):
        owner = at(step + 1 if side == LEFT else -step - 1)
        ref = out.at[chunk(c), pl.ds(pl.multiple_of(owner * width, 128), width)]
        pltpu.make_async_remote_copy(
            src_ref=ref, dst_ref=ref, send_sem=send_sem.at[1, side, step], recv_sem=ag_sem.at[side, step, c],
            device_id={AXIS: near[side]}, device_id_type=pl.DeviceIdType.MESH,
        ).wait_recv()

    low, high = tuple(range(CHUNKS // 2)), tuple(range(CHUNKS // 2, CHUNKS))
    first = {LEFT: low, RIGHT: high}

    def compute(offset):
        b = place[offset]
        down(b).wait()
        term[b] = jnp.dot(hid[...], wd[b], preferred_element_type=jnp.float32)

    def offset_of(side, step):
        return (-(half - step) if side == LEFT else half - step) if step else half

    def send_plain(side, step, c):
        b = place[offset_of(side, step)]
        sbuf[side, step, chunk(c)] = term[b, chunk(c)].astype(jnp.bfloat16)
        sum_copy(side, step, c).start()

    def send_sum(side, step, c):
        b = place[offset_of(side, step)]
        sum_copy(side, step - 1, c).wait_recv()
        total = term[b, chunk(c)] + rbuf[side, step - 1, chunk(c)].astype(jnp.float32)
        sbuf[side, step, chunk(c)] = total.astype(jnp.bfloat16)
        sum_copy(side, step, c).start()

    compute(half)
    pl.semaphore_wait(barrier, 2)
    for k in range(CHUNKS // 2):
        for side in (LEFT, RIGHT):
            send_plain(side, 0, first[side][k])
    last = {side: [c for c in range(CHUNKS) if c not in first[side]] for side in first}
    seq = {side: last[side] + list(first[side]) for side in first}
    for side in (LEFT, RIGHT):
        compute(offset_of(side, 1))
        for c in last[side]:
            send_plain(side, 1, c)
    for k in range(CHUNKS // 2):
        for side in (LEFT, RIGHT):
            send_sum(side, 1, first[side][k])
    for step in range(2, half):
        compute(offset_of(LEFT, step))
        send_sum(LEFT, step, seq[LEFT][0])
        compute(offset_of(RIGHT, step))
        send_sum(RIGHT, step, seq[RIGHT][0])
        for k in range(1, CHUNKS):
            for side in (LEFT, RIGHT):
                send_sum(side, step, seq[side][k])
    compute(0)

    mine = pl.ds(pl.multiple_of(me * width, 128), width)
    for c in range(CHUNKS):
        for side in (LEFT, RIGHT):
            sum_copy(side, half - 1, c).wait_recv()
        total = (
            term[place[0], chunk(c)]
            + rbuf[LEFT, half - 1, chunk(c)].astype(jnp.float32)
            + rbuf[RIGHT, half - 1, chunk(c)].astype(jnp.float32)
        )
        out[chunk(c), mine] = total.astype(jnp.bfloat16)
        for side in (LEFT, RIGHT):
            gather_copy(side, 0, c).start()
    for step in range(1, half):
        for k in range(CHUNKS):
            for side in (LEFT, RIGHT):
                c = (list(first[side]) + last[side])[k] if step >= half - 2 else k
                arrived(side, step - 1, c)
                if step < half - 1 or c in first[side]:
                    gather_copy(side, step, c).start()
    for side in (LEFT, RIGHT):
        for c in first[side]:
            arrived(side, half - 1, c)

    for side in (LEFT, RIGHT):
        for step in range(half):
            some = pl.ds(first[side][0] * cr, len(first[side]) * cr)
            part = some if step == 0 else pl.ds(0, rows)
            pltpu.make_async_remote_copy(
                src_ref=sbuf.at[side, step, part], dst_ref=rbuf.at[side, step, part],
                send_sem=send_sem.at[0, side, step], recv_sem=rs_sem.at[side, step, 0],
                device_id={AXIS: near[side]}, device_id_type=pl.DeviceIdType.MESH,
            ).wait_send()
            part = some if step == half - 1 else pl.ds(0, rows)
            ref = out.at[part, mine]
            pltpu.make_async_remote_copy(
                src_ref=ref, dst_ref=ref,
                send_sem=send_sem.at[1, side, step], recv_sem=ag_sem.at[side, step, 0],
                device_id={AXIS: near[side]}, device_id_type=pl.DeviceIdType.MESH,
            ).wait_send()


def solution(mesh):
    n = mesh.shape[AXIS]

    def step(x, w_gate, w_up, w_down):
        rows, model = x.shape
        depth = w_gate.shape[1]
        width, half = model // n, n // 2
        hbm = pl.BlockSpec(memory_space=pltpu.HBM)
        return pl.pallas_call(
            functools.partial(kernel, n),
            out_shape=jax.ShapeDtypeStruct((rows, model), jnp.bfloat16),
            in_specs=[hbm] * 4,
            out_specs=pl.BlockSpec(memory_space=pltpu.VMEM),
            scratch_shapes=[
                pltpu.VMEM((rows, model), jnp.bfloat16),
                pltpu.VMEM((SLOTS, model, SLAB), jnp.bfloat16),
                pltpu.VMEM((SLOTS, model, SLAB), jnp.bfloat16),
                pltpu.VMEM((n, depth, width), jnp.bfloat16),
                pltpu.VMEM((rows, depth), jnp.bfloat16),
                pltpu.VMEM((n, rows, width), jnp.float32),
                pltpu.VMEM((2, half, rows, width), jnp.bfloat16),
                pltpu.VMEM((2, half, rows, width), jnp.bfloat16),
                pltpu.SemaphoreType.DMA,
                pltpu.SemaphoreType.DMA((SLOTS,)),
                pltpu.SemaphoreType.DMA((SLOTS,)),
                pltpu.SemaphoreType.DMA((n,)),
                pltpu.SemaphoreType.DMA((2, 2, half)),
                pltpu.SemaphoreType.DMA((2, half, CHUNKS)),
                pltpu.SemaphoreType.DMA((2, half, CHUNKS)),
            ],
            compiler_params=pltpu.CompilerParams(
                collective_id=0, has_side_effects=True, vmem_limit_bytes=67_000_000
            ),
            cost_estimate=pl.CostEstimate(
                flops=6 * rows * model * depth, bytes_accessed=6 * model * depth, transcendentals=rows * depth
            ),
        )(x, w_gate, w_up, w_down)

    return jax.shard_map(
        step,
        mesh=mesh,
        in_specs=(P("dp", None), P(None, "tp"), P(None, "tp"), P("tp", None)),
        out_specs=P("dp", None),
        check_vma=False,
    )
```

time: 132 us -> 66.2 us (0.50)
  waiting for transfers between devices: 74.9 us -> 0 us
  Pallas kernels: 0 us -> 63.6 us
  matrix products: 40 us -> 0 us
  between operations: 13.4 us -> 0.01 us
    psum x1 -> x0, waiting for transfers between devices: 74.8 us -> none  [step(): return lax.psum(term, 'tp')]
    pallas_call x0 -> x1, Pallas kernels: none -> 63.6 us  [step(): pl.pallas_call(functools.partial(kernel, n), out_shape=jax.ShapeDtypeStru...]
    dot_general x2 -> x0, matrix products: 40 us -> none  [the longest x1 26.3 us: step(): jnp.dot(hidden, w_down, preferred_element_type=jnp.float32)]
    unnamed x5 -> x1, local copies, waits for them, and re-layouts: 3.77 us -> 2.46 us
  transfers between devices with their start and end apart: 1 -> 0, of which waited for: 1 -> 0; matrix products, arithmetic and copies ran while one was open for 0% -> 0% of each run, Pallas kernels for 0% -> 0%
where the time goes in v1:
time: 66.2 us; the launch traced here: 66.1 us
  Pallas kernels  63.6 us (96%)
  local copies, waits for them, and re-layouts  2.46 us (4%)
    pallas_call x1, Pallas kernels, step(): pl.pallas_call(functools.partial(kernel, n), out_shape=jax.ShapeDtypeStru...  63.6 us
    unnamed x1, local copies, waits for them, and re-layouts  2.46 us

profile of v1, /device:TPU:22, one launch (start us, length us, event | category | flops | bytes accessed | tf_op | source)
XLA Modules:
  0.0 66.1 jit_solution(9755654578141091668)
XLA Ops:
  0.0 63.6 %shard_map.46 = bf16[128,5120]{1,0:T(8,128)(2,1)} custom-call(bf16[128,5120]{1,0:T(8,128)(2,1)} %x_hbm.1, bf16[5120,3456]{1,0:T(8,128)(2,1)} %g_hbm.1, bf16[5120,3456]{1,0:T(8,128)(2,1)} %u_hbm.1, bf16[3456,5120]{1,0:T(8,128)(2,1)} %d_hbm.1), custom_call_target="tpu_custom_call" | custom-call | flops 13589544960 | bytes 106168320 | tf_op jit(solution)/shard_map/pallas_call | solution.py:225
  63.6 2.5 %copy.6 = bf16[128,5120]{1,0:T(8,128)(2,1)} copy(bf16[128,5120]{1,0:T(8,128)(2,1)} %shard_map.46) | data formatting | bytes 2621440

commit v2 on v0

v2 whole, which is shorter than its diff:
```python
import contextlib
import functools

import jax
import jax.numpy as jnp
from jax import lax
from jax.experimental import pallas as pl
from jax.experimental.pallas import tpu as pltpu
from jax.sharding import PartitionSpec as P

AXIS = "tp"
SLAB = 256
SLOTS = 3
DOWN_SLOTS = 5
AHEAD = 3
BULK = 1
CHUNKS = 8
FIRST = 3
LEFT, RIGHT = 0, 1
PROFILE = False

ORDER = (
    0, 1001, 1107, 1000, 1106, 1105, 1002, 1103, 1104, 1, 1016, 1017, 1015, 2, 1111, 1014,
    1110, 1011, 1010, 1013, 1117, 1116, 1012, 3, 1115, 1026, 1114, 1027, 1112, 1025, 1113, 4,
    1121, 1021, 1020, 1024, 1120, 1127, 5, 1023, 1125, 1022, 1126, 6, 1124, 1123, 1037, 1122,
    1131, 1031, 1130, 1030, 1137, 1036, 1135, 1035, 1034, 1136, 7, 1134, 1033, 1133, 1032, 1132,
    2001, 2000, 2007, 2005, 2006, 2004, 2003, 2002, 3011, 3111, 3010, 3110, 3017, 3117, 3015, 3115,
    3016, 3116, 3014, 3114, 3013, 3113, 3012, 3112, 3021, 3121, 3020, 3120, 3027, 3127, 3025, 3125,
    3026, 3126, 3024, 3124, 3023, 3123, 3022, 3122, 3031, 3137, 3030, 3135, 3034, 3136, 3033, 3032,
)


def scope(name):
    return jax.named_scope(name) if PROFILE else contextlib.nullcontext()


def block_order(half):
    order = [half]
    for k in range(half - 1, 0, -1):
        order += [-k, k]
    return order + [0]


def offset_of(half, side, step):
    return (step - half if side == LEFT else half - step) if step else half


def decode(code):
    kind, rest = divmod(code, 1000)
    if kind == 0:
        return ("dot", rest)
    if kind == 2:
        return ("own", rest)
    return ("sum" if kind == 1 else "pass", rest // 100, rest // 10 % 10, rest % 10)


def plan(n):
    half = n // 2
    steps = [decode(code) for code in ORDER]
    first = {LEFT: range(FIRST), RIGHT: range(FIRST, CHUNKS)}

    def sent(op):
        if op[0] == "own":
            return [("pass", side, 0, op[1]) for side in (LEFT, RIGHT)]
        return [op] if op[0] in ("sum", "pass") else []

    def waited(op):
        if op[0] == "own":
            return [("sum", side, half - 1, op[1]) for side in (LEFT, RIGHT)]
        if op[0] == "pass":
            return [("pass", op[1], op[2] - 1, op[3])]
        if op[0] == "sum" and (op[2] > 1 or (op[2] == 1 and op[3] in first[op[1]])):
            return [("sum", op[1], op[2] - 1, op[3])]
        return []

    starts = {m: i for i, op in enumerate(steps) for m in sent(op)}
    ends = {m: i for i, op in enumerate(steps) for m in waited(op)}
    known = [dict.fromkeys(range(-half, half + 1), -1) for _ in steps]
    change = True
    while change:
        change = False
        for i, op in enumerate(steps):
            new = dict(known[i - 1]) if i else dict(known[0])
            new[0] = i
            for m in waited(op):
                away = 1 if m[1] == LEFT else -1
                for o, value in known[starts[m]].items():
                    if o + away in new:
                        new[o + away] = max(new[o + away], value)
            if new != known[i]:
                known[i], change = new, True
    semaphores, last = {}, []
    for m in sorted((m for m in starts if m in ends), key=lambda m: starts[m]):
        if m[0] == "sum" and m[2] == half - 1 and m[1] == RIGHT:
            continue
        pair = [m, ("sum", RIGHT, half - 1, m[3])] if m[0] == "sum" and m[2] == half - 1 else [m]
        for k, before in enumerate(last):
            if all(known[starts[x] - 1].get(-1 if x[1] == LEFT else 1, -1) >= before for x in pair):
                break
        else:
            k = len(last)
            last.append(None)
        last[k] = ends[m]
        for x in pair:
            semaphores[x] = k
    for m in starts:
        semaphores.setdefault(m, len(last))
    return steps, first, semaphores


def kernel(n, x_hbm, g_hbm, u_hbm, d_hbm, out, xb, gb, ub, wd, hid, early, term, sbuf, rbuf,
           x_sem, g_sem, u_sem, t_sem, d_sem, send_sem, recv_sem):
    rows, width = x_hbm.shape[0], d_hbm.shape[1] // n
    depth = g_hbm.shape[1]
    full, rest = depth // SLAB, depth % SLAB
    half = n // 2
    me = lax.axis_index(AXIS)
    near = {LEFT: lax.rem(me + n - 1, n), RIGHT: lax.rem(me + 1, n)}
    cr = rows // CHUNKS
    order = block_order(half)
    place = {o: b for b, o in enumerate(order)}
    steps, first, semaphores = plan(n)

    def at(offset):
        return lax.rem(me + offset + n, n)

    def slab(i):
        if isinstance(i, int) and i == 0 and rest:
            cols, size = pl.ds(full * SLAB, rest), rest
        else:
            cols, size = pl.ds(pl.multiple_of((i - lead) * SLAB, 128), SLAB), SLAB
        slot = i % SLOTS if isinstance(i, int) else lax.rem(i, SLOTS)
        dst = (slot, slice(None), pl.ds(0, size))
        return (
            pltpu.make_async_copy(g_hbm.at[:, cols], gb.at[dst], g_sem.at[slot]),
            pltpu.make_async_copy(u_hbm.at[:, cols], ub.at[dst], u_sem.at[slot]),
        )

    def parts(size, share):
        cut = int(size * share) // 256 * 256
        return pl.ds(0, cut), pl.ds(cut, size - cut)

    def final_slab():
        cols = pl.ds((full - 1) * SLAB, SLAB)
        slot = (slabs - 1) % SLOTS
        for k, part in enumerate(parts(x_hbm.shape[1], 0.5)):
            yield (
                part,
                pltpu.make_async_copy(g_hbm.at[part, cols], gb.at[slot, part], t_sem.at[0, k]),
                pltpu.make_async_copy(u_hbm.at[part, cols], ub.at[slot, part], t_sem.at[1, k]),
            )

    def down(b):
        cols = pl.ds(pl.multiple_of(at(order[b]) * width, 128), width)
        slot = b % DOWN_SLOTS
        pieces = parts(depth, 0.75) if b == 0 else [pl.ds(0, depth)]
        return [
            (part, pltpu.make_async_copy(d_hbm.at[part, cols], wd.at[slot, part], d_sem.at[DOWN_SLOTS if k else slot]))
            for k, part in enumerate(pieces)
        ]

    def start_down(b):
        for _, c in down(b):
            c.start(priority=BULK)

    lead = 1 if rest else 0
    slabs = full + lead
    x_copy = pltpu.make_async_copy(x_hbm, xb, x_sem)
    x_copy.start()
    for i in range(SLOTS):
        for c in slab(i):
            c.start()

    barrier = pltpu.get_barrier_semaphore()
    for side in (LEFT, RIGHT):
        pl.semaphore_signal(barrier, inc=1, device_id={AXIS: near[side]}, device_id_type=pl.DeviceIdType.MESH)

    with scope("xw"):
        x_copy.wait()

    def activate(gate, up):
        return (jax.nn.silu(gate) * up).astype(jnp.bfloat16)

    def dot(a, b):
        return jnp.dot(a, b, preferred_element_type=jnp.float32)

    if rest:
        for c in slab(0):
            c.wait()
        hid[:, full * SLAB :] = activate(dot(xb[...], gb[0, :, :rest]), dot(xb[...], ub[0, :, :rest]))
        for c in slab(SLOTS):
            c.start()

    @pl.loop(lead, slabs - 1)
    def _(i):
        slot = lax.rem(i, SLOTS)
        with scope("h"):
            for c in slab(i):
                c.wait()
            cols = pl.ds(pl.multiple_of((i - lead) * SLAB, 128), SLAB)
            hid[:, cols] = activate(dot(xb[...], gb[slot]), dot(xb[...], ub[slot]))

        @pl.when(i + SLOTS < slabs - 1)
        def _():
            for c in slab(i + SLOTS):
                c.start()

        @pl.when(i + SLOTS == slabs - 1)
        def _():
            for _, *both in final_slab():
                for c in both:
                    c.start()
            start_down(0)

        for b in range(1, AHEAD):
            @pl.when(i + SLOTS == slabs - 1 + b)
            def _():
                start_down(b)

    slot = (slabs - 1) % SLOTS
    for part, *both in final_slab():
        with scope("hw"):
            for c in both:
                c.wait()
        with scope("hr"):
            gate, up = dot(xb[:, part], gb[slot, part]), dot(xb[:, part], ub[slot, part])
            if part.start == 0:
                early[0], early[1] = gate, up
    with scope("hs"):
        hid[:, (full - 1) * SLAB : full * SLAB] = activate(early[0] + gate, early[1] + up)

    def chunk(c):
        return pl.ds(c * cr, cr)

    def remote(src, dst, sems, recv, side):
        return pltpu.make_async_remote_copy(
            src_ref=src,
            dst_ref=dst,
            send_sem=sems,
            recv_sem=recv,
            device_id={AXIS: near[side]},
            device_id_type=pl.DeviceIdType.MESH,
        )

    def sum_copy(side, step, c):
        return remote(
            sbuf.at[side, step, chunk(c)], rbuf.at[side, step, chunk(c)],
            send_sem, recv_sem.at[semaphores["sum", side, step, c]], side,
        )

    def columns(offset):
        return pl.ds(pl.multiple_of(at(offset) * width, 128), width)

    def pass_copy(side, step, c, hops=0):
        ref = out.at[chunk(c), columns(step + hops if side == LEFT else -step - hops)]
        return remote(ref, ref, send_sem, recv_sem.at[semaphores["pass", side, step, c]], side)

    met = False
    for op in steps:
        if op[0] == "dot":
            b = op[1]
            for k, (part, copy) in enumerate(down(b)):
                with scope(f"w{b}"):
                    copy.wait()
                if k == 0 and b + AHEAD < n:
                    start_down(b + AHEAD)
                with scope(f"d{b}"):
                    some = dot(hid[:, part], wd[b % DOWN_SLOTS, part])
                    term[b] = term[b] + some if k else some
        elif op[0] == "sum":
            _, side, step, c = op
            if not met:
                pl.semaphore_wait(barrier, 2)
                met = True
            total = term[place[offset_of(half, side, step)], chunk(c)]
            if step > 1 or (step == 1 and c in first[side]):
                with scope(f"r{side}{step}{c}"):
                    sum_copy(side, step - 1, c).wait_recv()
                total = total + rbuf[side, step - 1, chunk(c)].astype(jnp.float32)
            sbuf[side, step, chunk(c)] = total.astype(jnp.bfloat16)
            sum_copy(side, step, c).start()
        elif op[0] == "own":
            c = op[1]
            with scope(f"f{c}"):
                both = rbuf.at[:, half - 1, chunk(c)]
                remote(both, both, send_sem, recv_sem.at[semaphores["sum", LEFT, half - 1, c]], LEFT).wait_recv()
            total = term[place[0], chunk(c)]
            for side in (LEFT, RIGHT):
                total = total + rbuf[side, half - 1, chunk(c)].astype(jnp.float32)
            out[chunk(c), columns(0)] = total.astype(jnp.bfloat16)
            for side in (LEFT, RIGHT):
                pass_copy(side, 0, c).start()
        else:
            _, side, step, c = op
            with scope(f"a{side}{step}{c}"):
                pass_copy(side, step - 1, c, hops=1).wait_recv()
            pass_copy(side, step, c).start()

    with scope("z"):
        both = out.at[:, pl.ds(0, 2 * width)]
        remote(both, both, send_sem, recv_sem.at[max(semaphores.values())], LEFT).wait_recv()
    with scope("ws"):
        everything = term.at[pl.ds(0, n - 1)]
        remote(everything, everything, send_sem, recv_sem.at[0], LEFT).wait_send()


def solution(mesh):
    n = mesh.shape[AXIS]

    def step(x, w_gate, w_up, w_down):
        rows, model = x.shape
        depth = w_gate.shape[1]
        width, half = model // n, n // 2
        hbm = pl.BlockSpec(memory_space=pltpu.HBM)
        operands = [pltpu.with_memory_space_constraint(a, pltpu.HBM) for a in (x, w_gate, w_up, w_down)]
        return pl.pallas_call(
            functools.partial(kernel, n),
            out_shape=jax.ShapeDtypeStruct((rows, model), jnp.bfloat16),
            in_specs=[hbm] * 4,
            out_specs=pl.BlockSpec(memory_space=pltpu.VMEM),
            scratch_shapes=[
                pltpu.VMEM((rows, model), jnp.bfloat16),
                pltpu.VMEM((SLOTS, model, SLAB), jnp.bfloat16),
                pltpu.VMEM((SLOTS, model, SLAB), jnp.bfloat16),
                pltpu.VMEM((DOWN_SLOTS, depth, width), jnp.bfloat16),
                pltpu.VMEM((rows, depth), jnp.bfloat16),
                pltpu.VMEM((2, rows, SLAB), jnp.float32),
                pltpu.VMEM((n, rows, width), jnp.float32),
                pltpu.VMEM((2, half, rows, width), jnp.bfloat16),
                pltpu.VMEM((2, half, rows, width), jnp.bfloat16),
                pltpu.SemaphoreType.DMA,
                pltpu.SemaphoreType.DMA((SLOTS,)),
                pltpu.SemaphoreType.DMA((SLOTS,)),
                pltpu.SemaphoreType.DMA((2, 2)),
                pltpu.SemaphoreType.DMA((DOWN_SLOTS + 1,)),
                pltpu.SemaphoreType.DMA,
                pltpu.SemaphoreType.DMA((max(plan(n)[2].values()) + 1,)),
            ],
            compiler_params=pltpu.CompilerParams(
                collective_id=0, has_side_effects=True, vmem_limit_bytes=52_000_000
            ),
            cost_estimate=pl.CostEstimate(
                flops=6 * rows * model * depth, bytes_accessed=6 * model * depth, transcendentals=rows * depth
            ),
        )(*operands)

    return jax.shard_map(
        step,
        mesh=mesh,
        in_specs=(P("dp", None), P(None, "tp"), P(None, "tp"), P("tp", None)),
        out_specs=P("dp", None),
        check_vma=False,
    )
```

time: 132 us -> 60.6 us (0.46)
  waiting for transfers between devices: 74.9 us -> 0 us
  Pallas kernels: 0 us -> 59.4 us
  matrix products: 40 us -> 0 us
  between operations: 13.4 us -> 0.01 us
  local copies, waits for them, and re-layouts: 3.77 us -> 1.06 us
    psum x1 -> x0, waiting for transfers between devices: 74.8 us -> none  [step(): return lax.psum(term, 'tp')]
    pallas_call x0 -> x1, Pallas kernels: none -> 59.4 us  [step(): pl.pallas_call(functools.partial(kernel, n), out_shape=jax.ShapeDtypeStru...]
    dot_general x2 -> x0, matrix products: 40 us -> none  [the longest x1 26.3 us: step(): jnp.dot(hidden, w_down, preferred_element_type=jnp.float32)]
    unnamed x5 -> x1, local copies, waits for them, and re-layouts: 3.77 us -> 1.06 us
  transfers between devices with their start and end apart: 1 -> 0, of which waited for: 1 -> 0; matrix products, arithmetic and copies ran while one was open for 0% -> 0% of each run, Pallas kernels for 0% -> 0%
where the time goes in v2:
time: 60.6 us; the launch traced here: 60.5 us
  Pallas kernels  59.4 us (98%)
  local copies, waits for them, and re-layouts  1.06 us (2%)
    pallas_call x1, Pallas kernels, step(): pl.pallas_call(functools.partial(kernel, n), out_shape=jax.ShapeDtypeStru...  59.4 us

profile of v2, /device:TPU:22, one launch (start us, length us, event | category | flops | bytes accessed | tf_op | source)
XLA Modules:
  0.0 60.5 jit_solution(14527610970094446882)
XLA Ops:
  0.0 59.4 %shard_map.46 = bf16[128,5120]{1,0:T(8,128)(2,1)S(1)} custom-call(bf16[128,5120]{1,0:T(8,128)(2,1)} %x_hbm.1, bf16[5120,3456]{1,0:T(8,128)(2,1)} %g_hbm.1, bf16[5120,3456]{1,0:T(8,128)(2,1)} %u_hbm.1, bf16[3456,5120]{1,0:T(8,128)(2,1)} %d_hbm.1), custom_call_target="tpu_custom_call" | custom-call | flops 13589544960 | bytes 106168320 | tf_op jit(solution)/shard_map/pallas_call | solution.py:316
  59.4 1.1 %copy.6 = bf16[128,5120]{1,0:T(8,128)(2,1)} copy(bf16[128,5120]{1,0:T(8,128)(2,1)S(1)} %shard_map.46) | data formatting | bytes 2621440

commit v3 on v2

--- a/solution.py
+++ b/solution.py
@@ -13,6 +13,7 @@
 SLOTS = 3
 DOWN_SLOTS = 5
 AHEAD = 3
+SPLIT = {0: 0.75, 2: 0.5}
 BULK = 1
 CHUNKS = 8
 FIRST = 3
@@ -26,7 +27,7 @@
     1131, 1031, 1130, 1030, 1137, 1036, 1135, 1035, 1034, 1136, 7, 1134, 1033, 1133, 1032, 1132,
     2001, 2000, 2007, 2005, 2006, 2004, 2003, 2002, 3011, 3111, 3010, 3110, 3017, 3117, 3015, 3115,
     3016, 3116, 3014, 3114, 3013, 3113, 3012, 3112, 3021, 3121, 3020, 3120, 3027, 3127, 3025, 3125,
-    3026, 3126, 3024, 3124, 3023, 3123, 3022, 3122, 3031, 3137, 3030, 3135, 3034, 3136, 3033, 3032,
+    3026, 3126, 3024, 3124, 3023, 3123, 3022, 3122, 3031, 3137, 3030, 3135, 3134, 3136, 3033, 3032,
 )
 
 
@@ -153,10 +154,11 @@
     def down(b):
         cols = pl.ds(pl.multiple_of(at(order[b]) * width, 128), width)
         slot = b % DOWN_SLOTS
-        pieces = parts(depth, 0.75) if b == 0 else [pl.ds(0, depth)]
+        pieces = parts(depth, SPLIT[b]) if b in SPLIT else [pl.ds(0, depth)]
+        sems = [d_sem.at[slot]] + [d_sem.at[DOWN_SLOTS + i] for i, other in enumerate(SPLIT) if other == b]
         return [
-            (part, pltpu.make_async_copy(d_hbm.at[part, cols], wd.at[slot, part], d_sem.at[DOWN_SLOTS if k else slot]))
-            for k, part in enumerate(pieces)
+            (part, pltpu.make_async_copy(d_hbm.at[part, cols], wd.at[slot, part], sem))
+            for part, sem in zip(pieces, sems)
         ]
 
     def start_down(b):
@@ -332,7 +334,7 @@
                 pltpu.SemaphoreType.DMA((SLOTS,)),
                 pltpu.SemaphoreType.DMA((SLOTS,)),
                 pltpu.SemaphoreType.DMA((2, 2)),
-                pltpu.SemaphoreType.DMA((DOWN_SLOTS + 1,)),
+                pltpu.SemaphoreType.DMA((DOWN_SLOTS + len(SPLIT),)),
                 pltpu.SemaphoreType.DMA,
                 pltpu.SemaphoreType.DMA((max(plan(n)[2].values()) + 1,)),
             ],

time: 60.6 us -> 60.4 us (level)
  no operation moved by 1% of the time
where the time goes in v3:
time: 60.4 us; the launch traced here: 60.3 us
  Pallas kernels  59.3 us (98%)
  local copies, waits for them, and re-layouts  1.06 us (2%)
    pallas_call x1, Pallas kernels, step(): pl.pallas_call(functools.partial(kernel, n), out_shape=jax.ShapeDtypeStru...  59.3 us

profile of v3, /device:TPU:22, one launch (start us, length us, event | category | flops | bytes accessed | tf_op | source)
XLA Modules:
  0.0 60.3 jit_solution(458920909166292731)
XLA Ops:
  0.0 59.3 %shard_map.46 = bf16[128,5120]{1,0:T(8,128)(2,1)S(1)} custom-call(bf16[128,5120]{1,0:T(8,128)(2,1)} %x_hbm.1, bf16[5120,3456]{1,0:T(8,128)(2,1)} %g_hbm.1, bf16[5120,3456]{1,0:T(8,128)(2,1)} %u_hbm.1, bf16[3456,5120]{1,0:T(8,128)(2,1)} %d_hbm.1), custom_call_target="tpu_custom_call" | custom-call | flops 13589544960 | bytes 106168320 | tf_op jit(solution)/shard_map/pallas_call | solution.py:318
  59.3 1.1 %copy.6 = bf16[128,5120]{1,0:T(8,128)(2,1)} copy(bf16[128,5120]{1,0:T(8,128)(2,1)S(1)} %shard_map.46) | data formatting | bytes 2621440

commit v4 on v3

--- a/solution.py
+++ b/solution.py
@@ -13,7 +13,7 @@
 SLOTS = 3
 DOWN_SLOTS = 5
 AHEAD = 3
-SPLIT = {0: 0.75, 2: 0.5}
+SPLIT = {0: 0.75, 1: 0.5, 2: 0.5}
 BULK = 1
 CHUNKS = 8
 FIRST = 3
@@ -21,13 +21,13 @@
 PROFILE = False
 
 ORDER = (
-    0, 1001, 1107, 1000, 1106, 1105, 1002, 1103, 1104, 1, 1016, 1017, 1015, 2, 1111, 1014,
-    1110, 1011, 1010, 1013, 1117, 1116, 1012, 3, 1115, 1026, 1114, 1027, 1112, 1025, 1113, 4,
-    1121, 1021, 1020, 1024, 1120, 1127, 5, 1023, 1125, 1022, 1126, 6, 1124, 1123, 1037, 1122,
-    1131, 1031, 1130, 1030, 1137, 1036, 1135, 1035, 1034, 1136, 7, 1134, 1033, 1133, 1032, 1132,
-    2001, 2000, 2007, 2005, 2006, 2004, 2003, 2002, 3011, 3111, 3010, 3110, 3017, 3117, 3015, 3115,
-    3016, 3116, 3014, 3114, 3013, 3113, 3012, 3112, 3021, 3121, 3020, 3120, 3027, 3127, 3025, 3125,
-    3026, 3126, 3024, 3124, 3023, 3123, 3022, 3122, 3031, 3137, 3030, 3135, 3134, 3136, 3033, 3032,
+    0, 1001, 1105, 1107, 1106, 1104, 1000, 1002, 1, 1015, 1016, 1017, 1014, 1103, 2, 1111,
+    1110, 1011, 1010, 1013, 1117, 1115, 1012, 1116, 3, 1114, 1025, 1112, 1113, 1026, 1027, 4,
+    1121, 1021, 1020, 1024, 1120, 5, 1127, 1125, 1126, 1023, 6, 1124, 1022, 1122, 1123, 1037,
+    1131, 1031, 1130, 1030, 1137, 1036, 1035, 1135, 7, 1136, 1134, 1034, 1033, 1133, 1132, 1032,
+    2001, 2000, 2007, 2005, 2006, 2004, 2003, 2002, 3111, 3011, 3110, 3010, 3117, 3017, 3115, 3015,
+    3116, 3014, 3114, 3013, 3012, 3113, 3016, 3112, 3121, 3020, 3021, 3127, 3027, 3125, 3024, 3126,
+    3023, 3022, 3025, 3124, 3120, 3030, 3026, 3123, 3122, 3031, 3137, 3034, 3135, 3033, 3136, 3032,
 )
 
 

time: 60.4 us -> 60.6 us (level)
  no operation moved by 1% of the time
where the time goes in v4:
time: 60.6 us
  Pallas kernels  59.5 us (98%)
  local copies, waits for them, and re-layouts  1.06 us (2%)
    pallas_call x1, Pallas kernels, step(): pl.pallas_call(functools.partial(kernel, n), out_shape=jax.ShapeDtypeStru...  59.5 us

profile of v4, /device:TPU:22, one launch (start us, length us, event | category | flops | bytes accessed | tf_op | source)
XLA Modules:
  0.0 60.6 jit_solution(16737546273906096837)
XLA Ops:
  0.0 59.5 %shard_map.46 = bf16[128,5120]{1,0:T(8,128)(2,1)S(1)} custom-call(bf16[128,5120]{1,0:T(8,128)(2,1)} %x_hbm.1, bf16[5120,3456]{1,0:T(8,128)(2,1)} %g_hbm.1, bf16[5120,3456]{1,0:T(8,128)(2,1)} %u_hbm.1, bf16[3456,5120]{1,0:T(8,128)(2,1)} %d_hbm.1), custom_call_target="tpu_custom_call" | custom-call | flops 13589544960 | bytes 106168320 | tf_op jit(solution)/shard_map/pallas_call | solution.py:318
  59.5 1.1 %copy.6 = bf16[128,5120]{1,0:T(8,128)(2,1)} copy(bf16[128,5120]{1,0:T(8,128)(2,1)S(1)} %shard_map.46) | data formatting | bytes 2621440

commit v5 on v3

--- a/solution.py
+++ b/solution.py
@@ -27,7 +27,7 @@
     1131, 1031, 1130, 1030, 1137, 1036, 1135, 1035, 1034, 1136, 7, 1134, 1033, 1133, 1032, 1132,
     2001, 2000, 2007, 2005, 2006, 2004, 2003, 2002, 3011, 3111, 3010, 3110, 3017, 3117, 3015, 3115,
     3016, 3116, 3014, 3114, 3013, 3113, 3012, 3112, 3021, 3121, 3020, 3120, 3027, 3127, 3025, 3125,
-    3026, 3126, 3024, 3124, 3023, 3123, 3022, 3122, 3031, 3137, 3030, 3135, 3134, 3136, 3033, 3032,
+    3026, 3126, 3024, 3124, 3023, 3123, 3022, 3122, 3031, 3137, 3030, 3135, 3034, 3136, 3033, 3032,
 )
 
 

time: 60.4 us -> 60.3 us (level)
  no operation moved by 1% of the time
where the time goes in v5:
time: 60.3 us; the launch traced here: 60.2 us
  Pallas kernels  59.2 us (98%)
  local copies, waits for them, and re-layouts  1.06 us (2%)
    pallas_call x1, Pallas kernels, step(): pl.pallas_call(functools.partial(kernel, n), out_shape=jax.ShapeDtypeStru...  59.2 us

profile of v5, /device:TPU:22, one launch (start us, length us, event | category | flops | bytes accessed | tf_op | source)
XLA Modules:
  0.0 60.2 jit_solution(15204159308313552476)
XLA Ops:
  0.0 59.2 %shard_map.46 = bf16[128,5120]{1,0:T(8,128)(2,1)S(1)} custom-call(bf16[128,5120]{1,0:T(8,128)(2,1)} %x_hbm.1, bf16[5120,3456]{1,0:T(8,128)(2,1)} %g_hbm.1, bf16[5120,3456]{1,0:T(8,128)(2,1)} %u_hbm.1, bf16[3456,5120]{1,0:T(8,128)(2,1)} %d_hbm.1), custom_call_target="tpu_custom_call" | custom-call | flops 13589544960 | bytes 106168320 | tf_op jit(solution)/shard_map/pallas_call | solution.py:318
  59.2 1.1 %copy.6 = bf16[128,5120]{1,0:T(8,128)(2,1)} copy(bf16[128,5120]{1,0:T(8,128)(2,1)S(1)} %shard_map.46) | data formatting | bytes 2621440
